TPU v7x, 256 devices: a whole 4x4x8 slice. The times are simulated.
256 devices in a mesh: genome: 32 (over z, x_hi, core), samples: 8 (over x_lo, y).
Axes of the slice: x: 4 (x_hi: 2, x_lo: 2; x = x_hi * 2 + x_lo), y: 4, z: 8, core: 2. Of those that a mesh axis runs over, the one named last changes fastest.
Arguments:
- haplotypes: bfloat16 [16384, 32768], P('samples', 'genome'), may hold values from 0 to 1
- window_ends: int32 [32768], P(('genome', 'samples')), may hold values from 1 to 32768, as said below
Outputs:
- ld_score: float32 [32768], P(('genome', 'samples'))
- profile: float32 [2, 32768], P(None, ('genome', 'samples'))
Inputs may be any that keep to these rules, and one draw needn't show every extreme that they name: window_ends[v] - v lies between 1 and 1024 for every variant v, and equals 1024 at v = 0.
All inputs are finite; a program needn't handle non-finite values.
Results may differ from a plain program's by a relative error of at most 0.0013.
Values may be sent and summed in bfloat16 or wider, within the bound.
A program may use at most 64 MiB of HBM per device.

v0:
```python
import math

import jax
import jax.numpy as jnp
from jax import lax
from jax.sharding import PartitionSpec as P

WIN = 1024
TILE = 128


variance_floor = 0.01


def sent_to_all(x, axis):
    copies = jnp.broadcast_to(x, (lax.axis_size(axis), *x.shape))
    return lax.all_to_all(copies, axis, split_axis=0, concat_axis=0, tiled=True)


def over_copies(x, axis):
    everything = sent_to_all(x, axis)
    return jnp.sum(everything, axis=0)


def from_behind(block, axis, distance):
    devices = range(lax.axis_size(axis))
    route = [(i - distance, i) for i in devices if i - distance in devices]
    return lax.ppermute(block, axis, route)


def in_blocks(x, dim, peers):
    lengths = x.shape
    pieces = x.reshape(*lengths[:dim], peers, lengths[dim] // peers, *lengths[dim + 1 :])
    return jnp.moveaxis(pieces, dim, 0)


def sum_at_owner(x, axis, dim):
    pieces = in_blocks(x, dim, lax.axis_size(axis))
    arrived = lax.all_to_all(pieces, axis, split_axis=0, concat_axis=0, tiled=True)
    return arrived.sum(axis=0)


def all_in_one(x, axis):
    leaves = jax.tree.leaves(x)
    turns = sorted(range(len(leaves)), key=lambda k: -leaves[k].size)
    width = (1, *leaves[turns[0]].shape)[-1]
    lines = [
        jnp.pad(leaves[k].reshape(-1), (0, -leaves[k].size % width)).reshape(-1, width)
        for k in turns
    ]
    both, at, found = (sent_to_all(jnp.concatenate(lines), axis), 0, {})
    for k, line in zip(turns, lines):
        piece = both[:, at : at + len(line)].reshape(len(both), -1)
        found[k] = piece[:, : leaves[k].size].reshape(-1, *leaves[k].shape)
        at += len(line)
    numbers = iter(range(len(leaves)))
    return jax.tree.map(lambda _: found[next(numbers)], x)


def folded_in_pairs(pieces, combine):
    while len(jax.tree.leaves(pieces)[0]) > 1:
        pieces = jax.vmap(combine)(
            *(jax.tree.map(lambda part: part[side::2], pieces) for side in (0, 1))
        )
    return jax.tree.map(lambda part: part[0], pieces)


def carried_in(x, axis, combine, identity):
    peers, position = (lax.axis_size(axis), lax.axis_index(axis))
    passed = jnp.arange(peers) < position

    def kept(part, zero, own):
        part = jnp.where(
            passed.reshape(-1, *(1 for _ in own.shape)), part, jnp.asarray(zero, own.dtype)
        )
        return part

    pieces = all_in_one(x, axis)
    return folded_in_pairs(jax.tree.map(kept, pieces, identity, x), combine)


def standardize(alleles, frequency, inverse_sd):
    return ((alleles.astype(jnp.float32) - frequency) * inverse_sd).astype(jnp.bfloat16)


def transpose_product(left_side, right_side):
    return lax.dot_general(
        left_side, right_side, (((0,), (0,)), ((), ())), preferred_element_type=jnp.float32
    )


def window_mean(cross_sum, haplo_total, row_position, column_position, window_end):
    correlation = cross_sum / haplo_total
    inside = (column_position > row_position[:, None]) & (column_position < window_end[:, None])
    squares = jnp.sum(
        jnp.where(inside, correlation * correlation, jnp.zeros_like(correlation)), axis=1
    )
    counted = jnp.maximum(window_end - row_position - 1, 1).astype(jnp.float32)
    return squares / counted


def per_device(haplotypes, window_ends):
    sample_count = lax.axis_size("samples")
    genome_count = lax.axis_size("genome")
    block_width = haplotypes.shape[1]
    share_rows = block_width // sample_count
    haplo_total = float(haplotypes.shape[0] * sample_count)
    counts = over_copies(jnp.sum(haplotypes, axis=0, dtype=jnp.float32), "samples")
    frequency = counts / haplo_total
    inverse_sd = lax.rsqrt(jnp.maximum(frequency * (1.0 - frequency), variance_floor))
    standard = standardize(haplotypes, frequency, inverse_sd)
    next_edge = from_behind(standard, "genome", -1)
    extended = jnp.concatenate([standard, next_edge], axis=1)
    sample_index = lax.axis_index("samples")
    genome_index = lax.axis_index("genome")
    row_position = sample_index * share_rows + jnp.arange(share_rows, dtype=jnp.int32)

    def single(tile_index):
        tile_start = tile_index * TILE
        row_block = lax.dynamic_slice_in_dim(standard, tile_start, TILE, 1)
        column_block = lax.dynamic_slice_in_dim(extended, tile_start, TILE + WIN, 1)
        return transpose_product(row_block, column_block)

    tiles = lax.map(
        single, jnp.arange(share_rows * lax.axis_size("samples") // TILE, dtype=jnp.int32)
    )
    cross_sum = sum_at_owner(
        tiles.reshape(share_rows * lax.axis_size("samples"), TILE + WIN), "samples", 0
    )
    column_position = (
        row_position[:, None] // TILE * TILE + jnp.arange(TILE + WIN, dtype=jnp.int32)[None, :]
    )
    window_end = window_ends - genome_index * block_width
    ld_score = window_mean(cross_sum, haplo_total, row_position, column_position, window_end)
    log_rates = jnp.array(
        [math.log(0.5) / (4 * share_rows), math.log(0.1) / (block_width * genome_count)],
        jnp.float32,
    )
    steps_index = jnp.arange(share_rows, dtype=jnp.float32)
    lag_steps = steps_index[:, None] - steps_index[None, :]
    decay_matrix = jnp.where(
        lag_steps[None] >= 0.0,
        jnp.exp(jnp.maximum(lag_steps, 0.0)[None] * log_rates[:, None, None]),
        0.0,
    )
    local_sums = jnp.einsum("ktu,u->kt", decay_matrix, ld_score, precision=lax.Precision.HIGHEST)

    def combine(earlier, later):
        return (earlier[0] * jnp.exp(later[1] * log_rates) + later[0], earlier[1] + later[1])

    identity = (jnp.zeros(2, jnp.float32), jnp.zeros((), jnp.float32))
    element = (local_sums[:, -1], jnp.full((), share_rows, jnp.float32))
    group_prefix = carried_in(element, "samples", combine, identity)
    remaining = ((sample_count - 1 - sample_index) * share_rows).astype(jnp.float32)
    group_total = over_copies(local_sums[:, -1] * jnp.exp(remaining * log_rates), "samples")
    outer_prefix = carried_in(
        (group_total, jnp.full((), share_rows * sample_count, jnp.float32)),
        "genome",
        combine,
        identity,
    )
    incoming = combine(outer_prefix, group_prefix)
    smoothed = local_sums + incoming[0][:, None] * jnp.exp(
        (steps_index[None, :] + 1.0) * log_rates[:, None]
    )
    position = (genome_index * block_width + row_position).astype(jnp.float32) + 1.0
    profile = (
        smoothed
        * (-jnp.expm1(log_rates))[:, None]
        / -jnp.expm1(position[None, :] * log_rates[:, None])
    )
    return (ld_score, profile)


def solution(mesh):
    placed = (P("samples", "genome"), P(("genome", "samples")))
    return jax.shard_map(
        per_device,
        mesh=mesh,
        in_specs=placed,
        out_specs=(P(("genome", "samples")), P(None, ("genome", "samples"))),
        check_vma=False,
    )
```

profile of v0, /device:TPU:1, one launch (start us, length us, event | category | flops | bytes accessed | tf_op | source)
XLA Modules:
  0.0 232.8 jit_solution(17847677191685629503)
XLA Ops:
  0.6 2.9 %convert_reduce_fusion = f32[1024]{0:T(1024)S(1)} fusion(bf16[2048,1024]{1,0:T(8,128)(2,1)} %param.5), kind=kLoop, calls=%fused_computation.7 | loop fusion | flops 4193280 | bytes 4198400 | tf_op jit(solution)/shard_map/reduce_sum | solution.py:108
  3.5 10.8 %all_to_all.27 = f32[8,1,1024]{2,1,0:T(1,128)S(1)} all-to-all(f32[8,1,1024]{2,1,0:T(1,128)S(1)} %broadcast_in_dim.61), channel_id=1, replica_groups=mesh['genome'=32,'samples'=8] {'samples'}, dimensions={0} | all-to-all | bytes 65536 | tf_op jit(solution)/shard_map/all_to_all | solution.py:17
  14.4 5.4 %fusion.11 = bf16[2048,1024]{1,0:T(8,128)(2,1)} fusion(bf16[2048,1024]{1,0:T(8,128)(2,1)} %param.5, f32[1024]{0:T(1024)S(1)} %get-tuple-element.45, f32[1024]{0:T(1024)S(1)} %get-tuple-element.44), kind=kLoop, calls=%fused_computation.9 | loop fusion | flops 8388608 | bytes 8396800 | tf_op jit(solution)/shard_map/convert_element_type | solution.py:83
  19.8 4.0 %collective-permute-start = (bf16[2048,1024]{1,0:T(8,128)(2,1)}, bf16[2048,1024]{1,0:T(8,128)(2,1)}, u32[]{:S(2)}, u32[]{:S(2)}) collective-permute-start(bf16[2048,1024]{1,0:T(8,128)(2,1)} %fusion.11), channel_id=1, source_target_pairs={{8,0},{16,8},{24,16},{32,24},{40,32},{48,40},{56,48},{64,56},{72,6... | collective-permute-start | bytes 12582920 | tf_op jit(solution)/shard_map/ppermute | solution.py:28
  23.8 48.8 %collective-permute-done = bf16[2048,1024]{1,0:T(8,128)(2,1)} collective-permute-done((bf16[2048,1024]{1,0:T(8,128)(2,1)}, bf16[2048,1024]{1,0:T(8,128)(2,1)}, u32[]{:S(2)}, u32[]{:S(2)}) %collective-permute-start) | collective-permute-done | bytes 4194336 | tf_op jit(solution)/shard_map/ppermute | solution.py:28
  72.6 8.1 %pad_maximum_fusion = bf16[2048,2048]{1,0:T(8,128)(2,1)} fusion(bf16[2048,1024]{1,0:T(8,128)(2,1)} %collective-permute-done, bf16[2048,1024]{1,0:T(8,128)(2,1)} %fusion.11), kind=kLoop, calls=%fused_computation.10 | loop fusion | flops 16777216 | bytes 16777216 | tf_op jit(solution)/shard_map/concatenate | solution.py:113
  80.8 44.0 %while.10 = (s32[]{:T(128)}, f32[8,128,1152]{2,1,0:T(8,128)}, s32[8]{0:T(128)S(1)}, bf16[2048,1024]{1,0:T(8,128)(2,1)}, bf16[2048,2048]{1,0:T(8,128)(2,1)}, /*in...) while((s32[]{:T(128)}, f32[8,128,1152]{2,1,0:T(8,128)}, s32[8]{0:T(128)S(1)}, ...), condition=%wide.region_3.4_spmd, body=%wide.region_2.3_spmd.sunk | while | flops 603979776 | bytes 5833408 | solution.py:124
  80.8 0.6 dynamic_slice.23
  82.0 4.3 %fusion.38 = f32[8,128,1152]{2,1,0:T(8,128)} fusion(f32[8,128,1152]{2,1,0:T(8,128)} %get-tuple-element.100, s32[]{:T(128)} %get-tuple-element.99, bf16[2048,2048]{1,0:T(8,128)(2,1)} %get-tuple-element.113, s32[]{:T(128)S(6)} %select_n.59, bf16[2048,1024]{1,0:T(8,128)(2,1)} %get-tuple-element.112, s32[]{:T(128)S(6)} %select_n.60), kind=kOutput, calls=%fused_computation.3.clone.1 | convolution fusion | flops 603979776 | bytes 5833224 | tf_op jit(solution)/shard_map/while/body/eval_jaxpr/dot_general | solution.py:87
  86.3 0.6 dynamic_slice.23
  87.5 4.3 %fusion.38 = f32[8,128,1152]{2,1,0:T(8,128)} fusion(f32[8,128,1152]{2,1,0:T(8,128)} %get-tuple-element.100, s32[]{:T(128)} %get-tuple-element.99, bf16[2048,2048]{1,0:T(8,128)(2,1)} %get-tuple-element.113, s32[]{:T(128)S(6)} %select_n.59, bf16[2048,1024]{1,0:T(8,128)(2,1)} %get-tuple-element.112, s32[]{:T(128)S(6)} %select_n.60), kind=kOutput, calls=%fused_computation.3.clone.1 | convolution fusion | flops 603979776 | bytes 5833224 | tf_op jit(solution)/shard_map/while/body/eval_jaxpr/dot_general | solution.py:87
  91.8 0.6 dynamic_slice.23
  93.1 4.2 %fusion.38 = f32[8,128,1152]{2,1,0:T(8,128)} fusion(f32[8,128,1152]{2,1,0:T(8,128)} %get-tuple-element.100, s32[]{:T(128)} %get-tuple-element.99, bf16[2048,2048]{1,0:T(8,128)(2,1)} %get-tuple-element.113, s32[]{:T(128)S(6)} %select_n.59, bf16[2048,1024]{1,0:T(8,128)(2,1)} %get-tuple-element.112, s32[]{:T(128)S(6)} %select_n.60), kind=kOutput, calls=%fused_computation.3.clone.1 | convolution fusion | flops 603979776 | bytes 5833224 | tf_op jit(solution)/shard_map/while/body/eval_jaxpr/dot_general | solution.py:87
  97.3 0.6 dynamic_slice.23
  98.6 4.3 %fusion.38 = f32[8,128,1152]{2,1,0:T(8,128)} fusion(f32[8,128,1152]{2,1,0:T(8,128)} %get-tuple-element.100, s32[]{:T(128)} %get-tuple-element.99, bf16[2048,2048]{1,0:T(8,128)(2,1)} %get-tuple-element.113, s32[]{:T(128)S(6)} %select_n.59, bf16[2048,1024]{1,0:T(8,128)(2,1)} %get-tuple-element.112, s32[]{:T(128)S(6)} %select_n.60), kind=kOutput, calls=%fused_computation.3.clone.1 | convolution fusion | flops 603979776 | bytes 5833224 | tf_op jit(solution)/shard_map/while/body/eval_jaxpr/dot_general | solution.py:87
  102.8 0.6 dynamic_slice.23
  104.1 4.2 %fusion.38 = f32[8,128,1152]{2,1,0:T(8,128)} fusion(f32[8,128,1152]{2,1,0:T(8,128)} %get-tuple-element.100, s32[]{:T(128)} %get-tuple-element.99, bf16[2048,2048]{1,0:T(8,128)(2,1)} %get-tuple-element.113, s32[]{:T(128)S(6)} %select_n.59, bf16[2048,1024]{1,0:T(8,128)(2,1)} %get-tuple-element.112, s32[]{:T(128)S(6)} %select_n.60), kind=kOutput, calls=%fused_computation.3.clone.1 | convolution fusion | flops 603979776 | bytes 5833224 | tf_op jit(solution)/shard_map/while/body/eval_jaxpr/dot_general | solution.py:87
  108.3 0.6 dynamic_slice.23
  109.5 4.2 %fusion.38 = f32[8,128,1152]{2,1,0:T(8,128)} fusion(f32[8,128,1152]{2,1,0:T(8,128)} %get-tuple-element.100, s32[]{:T(128)} %get-tuple-element.99, bf16[2048,2048]{1,0:T(8,128)(2,1)} %get-tuple-element.113, s32[]{:T(128)S(6)} %select_n.59, bf16[2048,1024]{1,0:T(8,128)(2,1)} %get-tuple-element.112, s32[]{:T(128)S(6)} %select_n.60), kind=kOutput, calls=%fused_computation.3.clone.1 | convolution fusion | flops 603979776 | bytes 5833224 | tf_op jit(solution)/shard_map/while/body/eval_jaxpr/dot_general | solution.py:87
  113.8 0.6 dynamic_slice.23
  115.0 4.2 %fusion.38 = f32[8,128,1152]{2,1,0:T(8,128)} fusion(f32[8,128,1152]{2,1,0:T(8,128)} %get-tuple-element.100, s32[]{:T(128)} %get-tuple-element.99, bf16[2048,2048]{1,0:T(8,128)(2,1)} %get-tuple-element.113, s32[]{:T(128)S(6)} %select_n.59, bf16[2048,1024]{1,0:T(8,128)(2,1)} %get-tuple-element.112, s32[]{:T(128)S(6)} %select_n.60), kind=kOutput, calls=%fused_computation.3.clone.1 | convolution fusion | flops 603979776 | bytes 5833224 | tf_op jit(solution)/shard_map/while/body/eval_jaxpr/dot_general | solution.py:87
  119.2 0.6 dynamic_slice.23
  120.5 4.3 %fusion.38 = f32[8,128,1152]{2,1,0:T(8,128)} fusion(f32[8,128,1152]{2,1,0:T(8,128)} %get-tuple-element.100, s32[]{:T(128)} %get-tuple-element.99, bf16[2048,2048]{1,0:T(8,128)(2,1)} %get-tuple-element.113, s32[]{:T(128)S(6)} %select_n.59, bf16[2048,1024]{1,0:T(8,128)(2,1)} %get-tuple-element.112, s32[]{:T(128)S(6)} %select_n.60), kind=kOutput, calls=%fused_computation.3.clone.1 | convolution fusion | flops 603979776 | bytes 5833224 | tf_op jit(solution)/shard_map/while/body/eval_jaxpr/dot_general | solution.py:87
  124.8 4.7 %all-to-all-start.1 = ((f32[8,128,1152]{2,1,0:T(8,128)}), f32[8,128,1152]{2,1,0:T(8,128)}, u32[]{:S(2)}, u32[]{:S(2)}) async-start(f32[8,128,1152]{2,1,0:T(8,128)} %get-tuple-element.29), calls=%async_computation.1 | async-start | bytes 9437184 | tf_op jit(solution)/shard_map/all_to_all | solution.py:39
  129.7 28.9 %all-to-all-done.1 = f32[8,128,1152]{2,1,0:T(8,128)} async-done(((f32[8,128,1152]{2,1,0:T(8,128)}), f32[8,128,1152]{2,1,0:T(8,128)}, u32[]{:S(2)}, u32[]{:S(2)}) %all-to-all-start.1) | async-done | bytes 4718624 | tf_op jit(solution)/shard_map/all_to_all | solution.py:39
  158.6 2.6 %reduce_sum.47 = f32[128,1152]{1,0:T(8,128)S(1)} reduce(f32[8,128,1152]{2,1,0:T(8,128)} %all-to-all-done.1, f32[]{:T(128)} %constant.71.clone.1), dimensions={0}, to_apply=%region_4.5 | reduce | flops 1032192 | bytes 5308420 | tf_op jit(solution)/shard_map/reduce_sum | solution.py:40
  161.3 0.3 select_reduce_fusion
  161.6 0.3 fusion.15
  161.9 0.2 slice_reduce_fusion
  162.1 0.6 broadcast_in_dim.66
  162.7 3.3 %all-to-all-start.2 = ((f32[8,1,2]{2,1,0:T(1,128)}), f32[8,1,2]{2,1,0:T(1,128)S(1)}, u32[]{:S(2)}, u32[]{:S(2)}) async-start(f32[8,1,2]{2,1,0:T(1,128)} %broadcast_in_dim.66), calls=%async_computation.2 | async-start | bytes 8192 | tf_op jit(solution)/shard_map/all_to_all | solution.py:17
  166.1 5.0 %all-to-all-done.2 = f32[8,1,2]{2,1,0:T(1,128)S(1)} async-done(((f32[8,1,2]{2,1,0:T(1,128)}), f32[8,1,2]{2,1,0:T(1,128)S(1)}, u32[]{:S(2)}, u32[]{:S(2)}) %all-to-all-start.2) | async-done | bytes 96 | tf_op jit(solution)/shard_map/all_to_all | solution.py:17
  171.1 0.6 broadcast_in_dim.109
  171.7 3.3 %all-to-all-start.4 = ((f32[8,2,2]{2,1,0:T(2,128)}), f32[8,2,2]{2,1,0:T(2,128)S(1)}, u32[]{:S(2)}, u32[]{:S(2)}) async-start(f32[8,2,2]{2,1,0:T(2,128)} %broadcast_in_dim.109), calls=%async_computation.4 | async-start | bytes 16384 | tf_op jit(solution)/shard_map/all_to_all | solution.py:17
  175.0 4.9 %all-to-all-done.4 = f32[8,2,2]{2,1,0:T(2,128)S(1)} async-done(((f32[8,2,2]{2,1,0:T(2,128)}), f32[8,2,2]{2,1,0:T(2,128)S(1)}, u32[]{:S(2)}, u32[]{:S(2)}) %all-to-all-start.4) | async-done | bytes 160 | tf_op jit(solution)/shard_map/all_to_all | solution.py:17
  180.0 0.6 broadcast_in_dim.67
  180.6 37.1 %all-to-all-start.3 = ((f32[32,2,2]{2,1,0:T(2,128)}), f32[32,2,2]{2,1,0:T(2,128)S(1)}, u32[]{:S(2)}, u32[]{:S(2)}) async-start(f32[32,2,2]{2,1,0:T(2,128)} %broadcast_in_dim.67), calls=%async_computation.3 | async-start | bytes 65536 | tf_op jit(solution)/shard_map/all_to_all | solution.py:17
  218.3 0.6 fusion.32
  220.4 7.0 %all-to-all-done.3 = f32[32,2,2]{2,1,0:T(2,128)S(1)} async-done(((f32[32,2,2]{2,1,0:T(2,128)}), f32[32,2,2]{2,1,0:T(2,128)S(1)}, u32[]{:S(2)}, u32[]{:S(2)}) %all-to-all-start.3) | async-done | bytes 544 | tf_op jit(solution)/shard_map/all_to_all | solution.py:17
  227.5 0.1 slice.127
  227.6 0.1 slice.130
  228.4 0.1 slice.124
  228.5 0.1 slice.128
  229.6 0.6 slice.143
  230.2 1.3 exponential_bitcast_fusion.1
  231.8 0.2 add_reduce_fusion.1
  231.9 0.2 add_reduce_fusion
  232.2 0.7 negate_divide_fusion
  (72 shorter events, 3.1 us)
Async XLA Ops:
  19.8 52.8 %collective-permute-start = (bf16[2048,1024]{1,0:T(8,128)(2,1)}, bf16[2048,1024]{1,0:T(8,128)(2,1)}, u32[]{:S(2)}, u32[]{:S(2)}) collective-permute-start(bf16[2048,1024]{1,0:T(8,128)(2,1)} %fusion.11), channel_id=1, source_target_pairs={{8,0},{16,8},{24,16},{32,24},{40,32},{48,40},{56,48},{64,56},{72,6... | collective-permute-start | bytes 12582920 | tf_op jit(solution)/shard_map/ppermute | solution.py:28
  124.8 4.9 %copy-start.1 = (s32[128]{0:T(128)S(1)}, s32[128]{0:T(128)}, u32[]{:S(2)}) copy-start(s32[128]{0:T(128)} %param.6) | copy-start | bytes 1540
  124.8 33.9 %all-to-all-start.1 = ((f32[8,128,1152]{2,1,0:T(8,128)}), f32[8,128,1152]{2,1,0:T(8,128)}, u32[]{:S(2)}, u32[]{:S(2)}) async-start(f32[8,128,1152]{2,1,0:T(8,128)} %get-tuple-element.29), calls=%async_computation.1 | async-start | bytes 9437184 | tf_op jit(solution)/shard_map/all_to_all | solution.py:39
  129.5 32.1 %copy-start = (f32[2]{0:T(128)S(1)}, f32[2]{0:T(128)}, u32[]{:S(2)}) copy-start(f32[2]{0:T(128)} %constant.77.clone) | copy-start | bytes 28
  129.5 36.5 %copy-start.5 = (f32[1,2]{1,0:T(1,128)S(1)}, f32[1,2]{1,0:T(1,128)}, u32[]{:S(2)}) copy-start(f32[1,2]{1,0:T(1,128)} %constant.76.clone.1) | copy-start | bytes 28
  129.5 45.5 %copy-start.4 = (f32[1,2]{1,0:T(1,128)S(1)}, f32[1,2]{1,0:T(1,128)}, u32[]{:S(2)}) copy-start(f32[1,2]{1,0:T(1,128)} %constant.75.clone.1) | copy-start | bytes 28
  129.5 102.6 %copy-start.2 = (f32[2]{0:T(128)S(1)}, f32[2]{0:T(128)}, u32[]{:S(2)}) copy-start(f32[2]{0:T(128)} %constant.80) | copy-start | bytes 28
  161.6 71.2 %copy-start.3 = (f32[128]{0:T(128)}, f32[128]{0:T(128)S(1)}, u32[]{:S(2)}) copy-start(f32[128]{0:T(128)S(1)} %convert_divide_fusion) | copy-start | bytes 1540
  162.7 8.4 %all-to-all-start.2 = ((f32[8,1,2]{2,1,0:T(1,128)}), f32[8,1,2]{2,1,0:T(1,128)S(1)}, u32[]{:S(2)}, u32[]{:S(2)}) async-start(f32[8,1,2]{2,1,0:T(1,128)} %broadcast_in_dim.66), calls=%async_computation.2 | async-start | bytes 8192 | tf_op jit(solution)/shard_map/all_to_all | solution.py:17
  171.7 8.3 %all-to-all-start.4 = ((f32[8,2,2]{2,1,0:T(2,128)}), f32[8,2,2]{2,1,0:T(2,128)S(1)}, u32[]{:S(2)}, u32[]{:S(2)}) async-start(f32[8,2,2]{2,1,0:T(2,128)} %broadcast_in_dim.109), calls=%async_computation.4 | async-start | bytes 16384 | tf_op jit(solution)/shard_map/all_to_all | solution.py:17
  180.6 46.8 %all-to-all-start.3 = ((f32[32,2,2]{2,1,0:T(2,128)}), f32[32,2,2]{2,1,0:T(2,128)S(1)}, u32[]{:S(2)}, u32[]{:S(2)}) async-start(f32[32,2,2]{2,1,0:T(2,128)} %broadcast_in_dim.67), calls=%async_computation.3 | async-start | bytes 65536 | tf_op jit(solution)/shard_map/all_to_all | solution.py:17
where the time goes:
time: 234 us; the launch traced here: 233 us
  waiting for transfers between devices  94.7 us (40%)
  starting transfers between devices  52.5 us (22%)
  matrix products  34.3 us (15%)
  other arithmetic  22.2 us (9%)
  local copies, waits for them, and re-layouts  10.9 us (5%)
  blocking collectives  10.8 us (5%)
  loops' own time  5.28 us (2%)
    ppermute x1, waiting for transfers between devices, from_behind(): return lax.ppermute(block, axis, route)  48.8 us
    all_to_all x3, starting transfers between devices, sent_to_all(): return lax.all_to_all(copies, axis, split_axis=0, concat_axis=0, tiled=True)  43.8 us
    dot_general x8, matrix products, transpose_product(): lax.dot_general(left_side, right_side, (((0,), (0,)), ((), ())), preferre...  34.1 us
    all_to_all x1, waiting for transfers between devices, sum_at_owner(): lax.all_to_all(pieces, axis, split_axis=0, concat_axis=0, tiled=True)  28.9 us
    all_to_all x3, waiting for transfers between devices, sent_to_all(): return lax.all_to_all(copies, axis, split_axis=0, concat_axis=0, tiled=True)  16.9 us
    all_to_all x1, blocking collectives, sent_to_all(): return lax.all_to_all(copies, axis, split_axis=0, concat_axis=0, tiled=True)  10.8 us
    concatenate x1, other arithmetic, per_device(): extended = jnp.concatenate([standard, next_edge], axis=1)  8.14 us
    convert_element_type x1, other arithmetic, standardize(): ((alleles.astype(jnp.float32) - frequency) * inverse_sd).astype(jnp.bfloa...  5.37 us
  transfers between devices with their start and end apart: 5, of which 5 were waited for; matrix products, arithmetic and copies ran while one was open for 1% of the time, Pallas kernels for 0%

commit v1 on v0

v1 whole, which is shorter than its diff:
```python
import math

import jax
import jax.numpy as jnp
from jax import lax
from jax.experimental import pallas as pl
from jax.experimental.pallas import tpu as pltpu
from jax.sharding import PartitionSpec as P

F32 = jnp.float32
BF16 = jnp.bfloat16
MESH = pl.DeviceIdType.MESH
VARIANCE_FLOOR = 0.01
T = 128
RING = 4


def rate_rows(shape, share, variants):
    row = lax.broadcasted_iota(jnp.int32, shape, 0)
    return jnp.where(row == 0, math.log(0.5) / (4 * share), math.log(0.1) / variants).astype(F32)


def one_minus_exp(x):
    series = jnp.ones_like(x)
    for order in range(9, 1, -1):
        series = 1.0 + series * x * (1.0 / order)
    return jnp.where(x > -0.5, -x * series, 1.0 - jnp.exp(x))


def transposed_dot(a, b):
    return lax.dot_general(a, b, (((0,), (0,)), ((), ())), preferred_element_type=F32)


def kernel_body(
    G, S, x_ref, ends_ref, ld_ref, prof_ref,
    raw, xs, halo, hs, sb, yr, xsend, xrecv, diag, own, score,
    cnt, cnts, tot, htot, stat, hstat, msg1, msgs1, msg2, msgs2, w1, w2,
    load_sem, halo_s, halo_r, cnt_s, cnt_r, stat_s, stat_r,
    y_s, y_r, x_s, x_r, m1_s, m1_r, m2_s, m2_r,
):
    rows = x_ref.shape[0]
    width = x_ref.shape[1]
    C = width // T
    haplos = float(rows * S)
    variants = width * G
    g = lax.axis_index("genome")
    s = lax.axis_index("samples")
    y = lax.rem(s, RING)
    half = s // RING
    partner = lax.rem(s + RING, S)
    before = lax.rem(g + G - 1, G)

    barrier = pltpu.get_barrier_semaphore()

    def greet_s(k, _):
        pl.semaphore_signal(barrier, inc=1, device_id={"samples": lax.rem(s + k, S)}, device_id_type=MESH)
        return 0

    def greet_g(k, _):
        pl.semaphore_signal(barrier, inc=1, device_id={"genome": lax.rem(g + k, G)}, device_id_type=MESH)
        return 0

    def load(c):
        return pltpu.make_async_copy(x_ref.at[:, pl.ds(c * T, T)], raw.at[c], load_sem.at[c])

    for c in range(C):
        load(c).start()
    lax.fori_loop(1, S, greet_s, 0)
    lax.fori_loop(1, G, greet_g, 0)

    ones = jnp.ones((16, rows), BF16)
    for c in range(C):
        load(c).wait()
        sums = jnp.dot(ones, raw[c], preferred_element_type=F32)
        cnt[pl.ds(c, 1), :] = sums[0:1, :]

    pl.semaphore_wait(barrier, S + G - 2)

    def halo_copy(c):
        return pltpu.make_async_remote_copy(
            src_ref=raw.at[c], dst_ref=halo.at[c], send_sem=halo_s.at[c], recv_sem=halo_r.at[c],
            device_id={"genome": before}, device_id_type=MESH,
        )

    def to_samples(src, dst, ss, rs):
        def copy(k):
            return pltpu.make_async_remote_copy(
                src_ref=src, dst_ref=dst.at[s], send_sem=ss.at[k], recv_sem=rs.at[s],
                device_id={"samples": lax.rem(s + k, S)}, device_id_type=MESH,
            )

        def arrival(k):
            peer = lax.rem(s + k, S)
            return pltpu.make_async_remote_copy(
                src_ref=src, dst_ref=dst.at[peer], send_sem=ss.at[k], recv_sem=rs.at[peer],
                device_id={"samples": peer}, device_id_type=MESH,
            )

        return copy, arrival

    cnt_copy, cnt_arrival = to_samples(cnt, cnts, cnt_s, cnt_r)
    for k in range(1, S):
        cnt_copy(k).start()
    for c in range(C):
        halo_copy(c).start()

    rates = rate_rows((8, T), T, variants)

    def weight1(k, _):
        ahead = (s - 1 - k).astype(F32)
        w1[k] = jnp.where(ahead >= 0.0, jnp.exp(jnp.maximum(ahead, 0.0) * T * rates), 0.0)
        return 0

    def weight2(k, _):
        ahead = (g - 1 - k).astype(F32)
        w2[k] = jnp.where(ahead >= 0.0, jnp.exp(jnp.maximum(ahead, 0.0) * width * rates), 0.0)
        return 0

    lax.fori_loop(0, S, weight1, 0)
    lax.fori_loop(0, G, weight2, 0)

    total = cnt[...]
    for k in range(1, S):
        cnt_arrival(k).wait_recv()
    for k in range(1, S):
        total = total + cnts[lax.rem(s + k, S)]
    tot[...] = total
    stat_copy = pltpu.make_async_remote_copy(
        src_ref=tot, dst_ref=htot, send_sem=stat_s, recv_sem=stat_r,
        device_id={"genome": before}, device_id_type=MESH,
    )
    stat_copy.start()

    def statistics(counts, out):
        frequency = counts / haplos
        out[0] = frequency
        out[1] = lax.rsqrt(jnp.maximum(frequency * (1.0 - frequency), VARIANCE_FLOOR))

    statistics(total, stat)

    STEP = 256

    def own_standard(c, _):
        f = stat[0, pl.ds(c, 1), :]
        d = stat[1, pl.ds(c, 1), :]
        for b in range(rows // STEP):
            part = raw[c, pl.ds(b * STEP, STEP), :].astype(F32)
            xs[pl.ds(b * STEP, STEP), pl.ds(pl.multiple_of(c * T, T), T)] = ((part - f) * d).astype(BF16)
        return 0

    lax.fori_loop(0, C, own_standard, 0)

    def y_copy(p, r):
        return pltpu.make_async_remote_copy(
            src_ref=sb.at[r, p], dst_ref=yr.at[y, r // RING, p],
            send_sem=y_s.at[r, p], recv_sem=y_r.at[y, r // RING, p],
            device_id={"samples": half * RING + r % RING}, device_id_type=MESH,
        )

    def y_send(p, r):
        @pl.when(y != r % RING)
        def _():
            y_copy(p, r).start()

    B = 2
    for q in range(C // B):
        product = transposed_dot(xs[:, q * B * T : (q + 1) * B * T], xs[:, : (q + 1) * B * T])
        for p in range(q * B, (q + 1) * B):
            at = (p - q * B) * T
            for r in range(p):
                sb[r, p] = product[at : at + T, r * T : (r + 1) * T].astype(BF16)
            diag[p] = product[at : at + T, p * T : (p + 1) * T]
            for r in range(p):
                y_send(p, r)

    def y_sum(j, p):
        value = sb[j * RING + y, p].astype(F32)
        for k in range(1, RING):
            slot = lax.rem(y + k, RING)
            pltpu.make_async_remote_copy(
                src_ref=sb.at[0, p], dst_ref=yr.at[slot, j, p],
                send_sem=y_s.at[0, p], recv_sem=y_r.at[slot, j, p],
                device_id={"samples": half * RING + slot}, device_id_type=MESH,
            ).wait_recv()
        for k in range(1, RING):
            value = value + yr[lax.rem(y + k, RING), j, p].astype(F32)
        return value

    r_own = half * RING + y
    r_other = (1 - half) * RING + y

    def x_copy(p):
        return pltpu.make_async_remote_copy(
            src_ref=xsend.at[p], dst_ref=xrecv.at[p], send_sem=x_s.at[p], recv_sem=x_r.at[p],
            device_id={"samples": partner}, device_id_type=MESH,
        )

    def other_tile(p, _):
        xsend[p] = y_sum(1 - half, p).astype(BF16)
        x_copy(p).start()
        return 0

    def own_tile(p, _):
        own[p] = y_sum(half, p)
        return 0

    lane = lax.broadcasted_iota(jnp.int32, (T, T), 1)
    sub = lax.broadcasted_iota(jnp.int32, (T, T), 0)

    def finish_tile(p, _):
        x_copy(p).wait_recv()
        value = (own[p] + xrecv[p].astype(F32)) * (1.0 / haplos)
        row = r_own * T + lane
        col = p * T + sub
        end = jnp.broadcast_to(ends_ref[...] - g * width, (T, T))
        inside = ((col > row) & (col < end)) | ((col < row) & (col + width < end))
        score[...] += jnp.sum(jnp.where(inside, value * value, 0.0), axis=0, keepdims=True)
        return 0

    score[...] = jnp.zeros_like(score)

    def halo_chunk(c):
        if c == 0:
            stat_copy.wait_recv()
            statistics(htot[...], hstat)
        halo_copy(c).wait_recv()
        f = hstat[0, c : c + 1, :]
        d = hstat[1, c : c + 1, :]
        for b in range(rows // STEP):
            part = halo[c, pl.ds(b * STEP, STEP), :].astype(F32)
            hs[pl.ds(b * STEP, STEP), :] = ((part - f) * d).astype(BF16)
        product = transposed_dot(hs[...], xs[:, c * T :])
        first = jnp.where(sub > lane, diag[c], product[:, :T])
        sb[c, c] = first.astype(BF16)
        for r in range(c + 1, C):
            sb[r, c] = product[:, (r - c) * T : (r - c + 1) * T].astype(BF16)
        for r in range(c, C):
            y_send(c, r)

    def halo_sums(c):
        @pl.when(r_other >= c)
        def _():
            other_tile(c, 0)

        @pl.when(r_own >= c)
        def _():
            own_tile(c, 0)

    def halo_finish(c):
        @pl.when(r_own >= c)
        def _():
            finish_tile(c, 0)

    SELF_AT = 2
    for c in range(C):
        halo_chunk(c)
        if c == SELF_AT:
            lax.fori_loop(r_other + 1, C, other_tile, 0)
            lax.fori_loop(r_own + 1, C, own_tile, 0)
            for k in range(SELF_AT):
                halo_sums(k)
        elif c > SELF_AT:
            halo_sums(c - 1)
        if c == SELF_AT + 1:
            lax.fori_loop(r_own + 1, C, finish_tile, 0)
            for k in range(SELF_AT):
                halo_finish(k)
        elif c > SELF_AT + 1:
            halo_finish(c - 2)
    halo_sums(C - 1)
    halo_finish(C - 2)
    halo_finish(C - 1)

    row = r_own * T + lax.broadcasted_iota(jnp.int32, (1, T), 1)
    counted = jnp.maximum(ends_ref[...] - g * width - row - 1, 1).astype(F32)
    ld = score[...] / counted
    ld_ref[...] = ld
    step = lax.broadcasted_iota(jnp.int32, (8, T), 1).astype(F32)
    msg1[...] = jnp.broadcast_to(
        jnp.sum(ld * jnp.exp((T - 1.0 - step) * rates), axis=1, keepdims=True), (8, T)
    )
    m1_copy, m1_arrival = to_samples(msg1, msgs1, m1_s, m1_r)
    for k in range(1, S):
        m1_copy(k).start()

    lag = (lane - sub).astype(F32)
    locals_ = []
    for rate in (math.log(0.5) / (4 * T), math.log(0.1) / variants):
        decay = jnp.where(lag >= 0.0, jnp.exp(jnp.maximum(lag, 0.0) * rate), 0.0)
        locals_.append(
            jnp.dot(jnp.broadcast_to(ld, (8, T)), decay, precision=lax.Precision.HIGHEST, preferred_element_type=F32)
        )
    local = jnp.where(lax.broadcasted_iota(jnp.int32, (8, T), 0) == 0, locals_[0], locals_[1])
    place = (g * width + s * T + 1).astype(F32) + step
    norm = one_minus_exp(rates) / one_minus_exp(place * rates)

    for k in range(1, S):
        m1_arrival(k).wait_recv()
    inner = w1[s] * msg1[...]
    whole = msg1[...] * jnp.exp((S - 1 - s).astype(F32) * T * rates)
    for k in range(1, S):
        peer = lax.rem(s + k, S)
        inner = inner + w1[peer] * msgs1[peer]
        whole = whole + msgs1[peer] * jnp.exp((S - 1 - peer).astype(F32) * T * rates)
    msg2[...] = whole

    def m2_copy(k):
        return pltpu.make_async_remote_copy(
            src_ref=msg2, dst_ref=msgs2.at[g], send_sem=m2_s.at[k], recv_sem=m2_r.at[g],
            device_id={"genome": lax.rem(g + k, G)}, device_id_type=MESH,
        )

    def m2_arrival(k):
        peer = lax.rem(g + k, G)
        return pltpu.make_async_remote_copy(
            src_ref=msg2, dst_ref=msgs2.at[peer], send_sem=m2_s.at[k], recv_sem=m2_r.at[peer],
            device_id={"genome": peer}, device_id_type=MESH,
        )

    def m2_start(k, _):
        m2_copy(k).start()
        return 0

    def m2_wait(k, _):
        m2_arrival(k).wait_recv()
        return 0

    lax.fori_loop(1, G, m2_start, 0)

    for c in range(C):
        halo_copy(c).wait_send()
        for r in range(C):
            @pl.when(y != r % RING)
            def _():
                y_copy(c, r).wait_send()
    stat_copy.wait_send()
    lax.fori_loop(0, C, lambda p, _: (x_copy(p).wait_send(), 0)[1], 0)
    for k in range(1, S):
        cnt_copy(k).wait_send()
        m1_copy(k).wait_send()

    lax.fori_loop(1, G, m2_wait, 0)
    outer = jnp.zeros((8, T), F32)
    for k in range(1, G):
        peer = lax.rem(g + k, G)
        outer = outer + w2[peer] * msgs2[peer]
    incoming = inner + outer * jnp.exp((s * T).astype(F32) * rates)
    smoothed = local + incoming * jnp.exp((step + 1.0) * rates)
    prof_ref[...] = (smoothed * norm)[:2]
    lax.fori_loop(1, G, lambda k, _: (m2_copy(k).wait_send(), 0)[1], 0)


def per_device(haplotypes, window_ends):
    G = lax.axis_size("genome")
    S = lax.axis_size("samples")
    rows, width = haplotypes.shape
    C = width // T
    dma = pltpu.SemaphoreType.DMA

    def body(*refs):
        kernel_body(G, S, *refs)

    ld, prof = pl.pallas_call(
        body,
        out_shape=(jax.ShapeDtypeStruct((1, T), F32), jax.ShapeDtypeStruct((2, T), F32)),
        in_specs=[pl.BlockSpec(memory_space=pl.ANY), pl.BlockSpec(memory_space=pltpu.VMEM)],
        out_specs=(pl.BlockSpec(memory_space=pltpu.VMEM), pl.BlockSpec(memory_space=pltpu.VMEM)),
        scratch_shapes=[
            pltpu.VMEM((C, rows, T), BF16),
            pltpu.VMEM((rows, width), BF16),
            pltpu.VMEM((C, rows, T), BF16),
            pltpu.VMEM((rows, T), BF16),
            pltpu.VMEM((C, C, T, T), BF16),
            pltpu.VMEM((RING, 2, C, T, T), BF16),
            pltpu.VMEM((C, T, T), BF16),
            pltpu.VMEM((C, T, T), BF16),
            pltpu.VMEM((C, T, T), F32),
            pltpu.VMEM((C, T, T), F32),
            pltpu.VMEM((1, T), F32),
            pltpu.VMEM((8, T), F32),
            pltpu.VMEM((S, 8, T), F32),
            pltpu.VMEM((8, T), F32),
            pltpu.VMEM((8, T), F32),
            pltpu.VMEM((2, 8, T), F32),
            pltpu.VMEM((2, 8, T), F32),
            pltpu.VMEM((8, T), F32),
            pltpu.VMEM((S, 8, T), F32),
            pltpu.VMEM((8, T), F32),
            pltpu.VMEM((G, 8, T), F32),
            pltpu.VMEM((S, 8, T), F32),
            pltpu.VMEM((G, 8, T), F32),
            dma((C,)), dma((C,)), dma((C,)), dma((S,)), dma((S,)), dma, dma,
            dma((C, C)), dma((RING, 2, C)), dma((C,)), dma((C,)),
            dma((S,)), dma((S,)), dma((G,)), dma((G,)),
        ],
        compiler_params=pltpu.CompilerParams(collective_id=0, has_side_effects=True),
        name="ld_scores",
    )(haplotypes, window_ends.reshape(1, T))
    return ld.reshape(T), prof


def solution(mesh):
    return jax.shard_map(
        per_device,
        mesh=mesh,
        in_specs=(P("samples", "genome"), P(("genome", "samples"))),
        out_specs=(P(("genome", "samples")), P(None, ("genome", "samples"))),
        check_vma=False,
    )
```

time: 234 us -> 109 us (0.47)
  Pallas kernels: 0 us -> 106 us
  waiting for transfers between devices: 94.7 us -> 0 us
  starting transfers between devices: 52.5 us -> 0 us
  matrix products: 34.3 us -> 0 us
  other arithmetic: 22.2 us -> 0 us
  blocking collectives: 10.8 us -> 0 us
  local copies, waits for them, and re-layouts: 10.9 us -> 2.36 us
  loops' own time: 5.28 us -> 0 us
    pallas_call x0 -> x1, Pallas kernels: none -> 106 us  [per_device(): pl.pallas_call(body, out_shape=(jax.ShapeDtypeStruct((1, T), F32), jax.Sh...]
    ppermute x1 -> x0, waiting for transfers between devices: 48.8 us -> none  [from_behind(): return lax.ppermute(block, axis, route)]
    all_to_all x4 -> x0, starting transfers between devices: 48.5 us -> none  [the longest x3 43.8 us: sent_to_all(): return lax.all_to_all(copies, axis, split_axis=0, concat_axis=0, tiled=True)]
    all_to_all x4 -> x0, waiting for transfers between devices: 45.8 us -> none  [the longest x1 28.9 us: sum_at_owner(): lax.all_to_all(pieces, axis, split_axis=0, concat_axis=0, tiled=True)]
    dot_general x9 -> x0, matrix products: 34.3 us -> none  [the longest x8 34.1 us: transpose_product(): lax.dot_general(left_side, right_side, (((0,), (0,)), ((), ())), preferre...]
    all_to_all x1 -> x0, blocking collectives: 10.8 us -> none  [sent_to_all(): return lax.all_to_all(copies, axis, split_axis=0, concat_axis=0, tiled=True)]
    concatenate x3 -> x0, other arithmetic: 8.16 us -> none  [the longest x1 8.14 us: per_device(): extended = jnp.concatenate([standard, next_edge], axis=1)]
    reduce_sum x5 -> x0, other arithmetic: 5.85 us -> none  [the longest x1 2.87 us: per_device(): jnp.sum(haplotypes, axis=0, dtype=jnp.float32)]
  transfers between devices with their start and end apart: 5 -> 0, of which waited for: 5 -> 0; matrix products, arithmetic and copies ran while one was open for 1% -> 0% of each run, Pallas kernels for 0% -> 0%
where the time goes in v1:
time: 109 us
  Pallas kernels  106 us (97%)
  local copies, waits for them, and re-layouts  2.36 us (2%)
    pallas_call x1, Pallas kernels, per_device(): pl.pallas_call(body, out_shape=(jax.ShapeDtypeStruct((1, T), F32), jax.Sh...  106 us
    unnamed x2, local copies, waits for them, and re-layouts  2.36 us

profile of v1, /device:TPU:1, one launch (start us, length us, event | category | flops | bytes accessed | tf_op | source)
XLA Modules:
  0.0 108.9 jit_solution(16131864742370901807)
XLA Ops:
  0.6 105.9 %ld_scores.1 = (f32[1,128]{1,0:T(1,128)}, f32[2,128]{1,0:T(2,128)}) custom-call(bf16[2048,1024]{1,0:T(8,128)(2,1)} %refs_0_.1, s32[1,128]{1,0:T(1,128)} %bitcast.2), custom_call_target="tpu_custom_call" | custom-call | tf_op jit(solution)/shard_map/ld_scores/pallas_call | solution.py:363
  106.6 1.1 %copy.6 = f32[128]{0:T(128)} copy(f32[128]{0:T(128)} %bitcast.3) | data formatting | bytes 1024
  107.7 1.2 %copy.7 = f32[2,128]{1,0:T(2,128)} copy(f32[2,128]{1,0:T(2,128)} %get-tuple-element.9) | data formatting | bytes 2048

commit v2 on v1

--- a/solution.py
+++ b/solution.py
@@ -12,6 +12,8 @@
 MESH = pl.DeviceIdType.MESH
 VARIANCE_FLOOR = 0.01
 T = 128
+FIRST = 2
+AHEAD = 2
 RING = 4
 
 
@@ -32,11 +34,11 @@
 
 
 def kernel_body(
-    G, S, x_ref, ends_ref, ld_ref, prof_ref,
-    raw, xs, halo, hs, sb, yr, xsend, xrecv, diag, own, score,
+    G, S, x_ref, ends_ref, out_ref,
+    raw, xs, halo, hs, sb, yr, hb, yh, last, xsend, xrecv, diag, own, score,
     cnt, cnts, tot, htot, stat, hstat, msg1, msgs1, msg2, msgs2, w1, w2,
     load_sem, halo_s, halo_r, cnt_s, cnt_r, stat_s, stat_r,
-    y_s, y_r, x_s, x_r, m1_s, m1_r, m2_s, m2_r,
+    y_s, y_r, h_s, h_r, d_s, d_r, x_s, x_r, m1_s, m1_r, m2_s, m2_r,
 ):
     rows = x_ref.shape[0]
     width = x_ref.shape[1]
@@ -101,7 +103,9 @@
     cnt_copy, cnt_arrival = to_samples(cnt, cnts, cnt_s, cnt_r)
     for k in range(1, S):
         cnt_copy(k).start()
-    for c in range(C):
+    for k in range(1, S):
+        cnt_copy(k).wait_send()
+    for c in range(FIRST):
         halo_copy(c).start()
 
     rates = rate_rows((8, T), T, variants)
@@ -130,6 +134,8 @@
         device_id={"genome": before}, device_id_type=MESH,
     )
     stat_copy.start()
+    for c in range(FIRST, AHEAD):
+        halo_copy(c).start()
 
     def statistics(counts, out):
         frequency = counts / haplos
@@ -150,17 +156,48 @@
 
     lax.fori_loop(0, C, own_standard, 0)
 
-    def y_copy(p, r):
-        return pltpu.make_async_remote_copy(
-            src_ref=sb.at[r, p], dst_ref=yr.at[y, r // RING, p],
-            send_sem=y_s.at[r, p], recv_sem=y_r.at[y, r // RING, p],
+    def y_copy(r):
+        size = C - 1 - r
+        return pltpu.make_async_remote_copy(
+            src_ref=sb.at[r, pl.ds(r + 1, size)], dst_ref=yr.at[y, r // RING, pl.ds(r + 1, size)],
+            send_sem=y_s.at[r], recv_sem=y_r.at[y, r // RING],
             device_id={"samples": half * RING + r % RING}, device_id_type=MESH,
         )
 
-    def y_send(p, r):
-        @pl.when(y != r % RING)
-        def _():
-            y_copy(p, r).start()
+    def y_arrival(slot, r):
+        size = C - 1 - r
+        return pltpu.make_async_remote_copy(
+            src_ref=sb.at[r, pl.ds(r + 1, size)], dst_ref=yr.at[slot, r // RING, pl.ds(r + 1, size)],
+            send_sem=y_s.at[r], recv_sem=y_r.at[slot, r // RING],
+            device_id={"samples": half * RING + slot}, device_id_type=MESH,
+        )
+
+    def h_copy(c, to):
+        low = 0 if c <= to else 1
+        return pltpu.make_async_remote_copy(
+            src_ref=hb.at[c, to, pl.ds(low, 2 - low)], dst_ref=yh.at[y, c, pl.ds(low, 2 - low)],
+            send_sem=h_s.at[c, to], recv_sem=h_r.at[y, c],
+            device_id={"samples": half * RING + to}, device_id_type=MESH,
+        )
+
+    def h_arrival(c, slot, low):
+        return pltpu.make_async_remote_copy(
+            src_ref=hb.at[c, 0, pl.ds(low, 2 - low)], dst_ref=yh.at[slot, c, pl.ds(low, 2 - low)],
+            send_sem=h_s.at[c, 0], recv_sem=h_r.at[slot, c],
+            device_id={"samples": half * RING + slot}, device_id_type=MESH,
+        )
+
+    def d_copy():
+        return pltpu.make_async_remote_copy(
+            src_ref=hb.at[C - 1, RING - 1, 1], dst_ref=last.at[s], send_sem=d_s, recv_sem=d_r.at[s],
+            device_id={"samples": S - 1}, device_id_type=MESH,
+        )
+
+    def d_arrival(k):
+        return pltpu.make_async_remote_copy(
+            src_ref=hb.at[C - 1, RING - 1, 1], dst_ref=last.at[k], send_sem=d_s, recv_sem=d_r.at[k],
+            device_id={"samples": k}, device_id_type=MESH,
+        )
 
     B = 2
     for q in range(C // B):
@@ -170,22 +207,42 @@
             for r in range(p):
                 sb[r, p] = product[at : at + T, r * T : (r + 1) * T].astype(BF16)
             diag[p] = product[at : at + T, p * T : (p + 1) * T]
-            for r in range(p):
-                y_send(p, r)
-
-    def y_sum(j, p):
+    for r in range(C - 1):
+        @pl.when(y != r % RING)
+        def _():
+            y_copy(r).start()
+
+    def self_sum(j, p):
         value = sb[j * RING + y, p].astype(F32)
-        for k in range(1, RING):
-            slot = lax.rem(y + k, RING)
-            pltpu.make_async_remote_copy(
-                src_ref=sb.at[0, p], dst_ref=yr.at[slot, j, p],
-                send_sem=y_s.at[0, p], recv_sem=y_r.at[slot, j, p],
-                device_id={"samples": half * RING + slot}, device_id_type=MESH,
-            ).wait_recv()
         for k in range(1, RING):
             value = value + yr[lax.rem(y + k, RING), j, p].astype(F32)
         return value
 
+    def halo_sum(j, c):
+        value = hb[c, y, j].astype(F32)
+        for k in range(1, RING):
+            value = value + yh[lax.rem(y + k, RING), c, j].astype(F32)
+        return value
+
+    def self_wait(j):
+        for r in range(C - 1):
+            @pl.when(j * RING + y == r)
+            def _():
+                for k in range(1, RING):
+                    y_arrival(lax.rem(y + k, RING), r).wait_recv()
+
+    def halo_wait(c):
+        if c < RING:
+            @pl.when(y >= c)
+            def _():
+                for k in range(1, RING):
+                    h_arrival(c, lax.rem(y + k, RING), 0).wait_recv()
+
+        @pl.when((y < c) & (y + RING >= c))
+        def _():
+            for k in range(1, RING):
+                h_arrival(c, lax.rem(y + k, RING), 1).wait_recv()
+
     r_own = half * RING + y
     r_other = (1 - half) * RING + y
 
@@ -196,12 +253,12 @@
         )
 
     def other_tile(p, _):
-        xsend[p] = y_sum(1 - half, p).astype(BF16)
+        xsend[p] = self_sum(1 - half, p).astype(BF16)
         x_copy(p).start()
         return 0
 
     def own_tile(p, _):
-        own[p] = y_sum(half, p)
+        own[p] = self_sum(half, p)
         return 0
 
     lane = lax.broadcasted_iota(jnp.int32, (T, T), 1)
@@ -209,13 +266,16 @@
 
     def finish_tile(p, _):
         x_copy(p).wait_recv()
-        value = (own[p] + xrecv[p].astype(F32)) * (1.0 / haplos)
+        add_squares(p, own[p] + xrecv[p].astype(F32))
+        return 0
+
+    def add_squares(p, value):
+        value = value * (1.0 / haplos)
         row = r_own * T + lane
         col = p * T + sub
         end = jnp.broadcast_to(ends_ref[...] - g * width, (T, T))
         inside = ((col > row) & (col < end)) | ((col < row) & (col + width < end))
         score[...] += jnp.sum(jnp.where(inside, value * value, 0.0), axis=0, keepdims=True)
-        return 0
 
     score[...] = jnp.zeros_like(score)
 
@@ -224,6 +284,9 @@
             stat_copy.wait_recv()
             statistics(htot[...], hstat)
         halo_copy(c).wait_recv()
+        if c + AHEAD < C:
+            halo_copy(c).wait_send()
+            halo_copy(c + AHEAD).start()
         f = hstat[0, c : c + 1, :]
         d = hstat[1, c : c + 1, :]
         for b in range(rows // STEP):
@@ -231,31 +294,44 @@
             hs[pl.ds(b * STEP, STEP), :] = ((part - f) * d).astype(BF16)
         product = transposed_dot(hs[...], xs[:, c * T :])
         first = jnp.where(sub > lane, diag[c], product[:, :T])
-        sb[c, c] = first.astype(BF16)
+        hb[c, c % RING, c // RING] = first.astype(BF16)
         for r in range(c + 1, C):
-            sb[r, c] = product[:, (r - c) * T : (r - c + 1) * T].astype(BF16)
-        for r in range(c, C):
-            y_send(c, r)
+            hb[c, r % RING, r // RING] = product[:, (r - c) * T : (r - c + 1) * T].astype(BF16)
+        if c == C - 1:
+            @pl.when(s != S - 1)
+            def _():
+                d_copy().start()
+            return
+        for to in range(RING):
+            if c <= to + RING:
+                @pl.when(y != to)
+                def _():
+                    h_copy(c, to).start()
 
     def halo_sums(c):
+        halo_wait(c)
+
         @pl.when(r_other >= c)
         def _():
-            other_tile(c, 0)
+            xsend[c] = halo_sum(1 - half, c).astype(BF16)
+            x_copy(c).start()
 
         @pl.when(r_own >= c)
         def _():
-            own_tile(c, 0)
+            own[c] = halo_sum(half, c)
 
     def halo_finish(c):
         @pl.when(r_own >= c)
         def _():
             finish_tile(c, 0)
 
-    SELF_AT = 2
+    SELF_AT = 3
     for c in range(C):
         halo_chunk(c)
         if c == SELF_AT:
+            self_wait(1 - half)
             lax.fori_loop(r_other + 1, C, other_tile, 0)
+            self_wait(half)
             lax.fori_loop(r_own + 1, C, own_tile, 0)
             for k in range(SELF_AT):
                 halo_sums(k)
@@ -267,14 +343,21 @@
                 halo_finish(k)
         elif c > SELF_AT + 1:
             halo_finish(c - 2)
-    halo_sums(C - 1)
     halo_finish(C - 2)
-    halo_finish(C - 1)
+
+    @pl.when(s == S - 1)
+    def _():
+        value = hb[C - 1, RING - 1, 1].astype(F32)
+        for k in range(S - 1):
+            d_arrival(k).wait_recv()
+        for k in range(S - 1):
+            value = value + last[k].astype(F32)
+        add_squares(C - 1, value)
 
     row = r_own * T + lax.broadcasted_iota(jnp.int32, (1, T), 1)
     counted = jnp.maximum(ends_ref[...] - g * width - row - 1, 1).astype(F32)
     ld = score[...] / counted
-    ld_ref[...] = ld
+    out_ref[0:1] = ld
     step = lax.broadcasted_iota(jnp.int32, (8, T), 1).astype(F32)
     msg1[...] = jnp.broadcast_to(
         jnp.sum(ld * jnp.exp((T - 1.0 - step) * rates), axis=1, keepdims=True), (8, T)
@@ -327,16 +410,29 @@
 
     lax.fori_loop(1, G, m2_start, 0)
 
-    for c in range(C):
+    for c in range(C - AHEAD, C):
         halo_copy(c).wait_send()
-        for r in range(C):
-            @pl.when(y != r % RING)
-            def _():
-                y_copy(c, r).wait_send()
+    for r in range(C - 1):
+        @pl.when(y != r % RING)
+        def _():
+            y_copy(r).wait_send()
+    for to in range(RING):
+        @pl.when(y != to)
+        def _():
+            for c in range(C - 1):
+                if c <= to + RING:
+                    h_copy(c, to).wait_send()
+
+    @pl.when(s != S - 1)
+    def _():
+        d_copy().wait_send()
+
     stat_copy.wait_send()
-    lax.fori_loop(0, C, lambda p, _: (x_copy(p).wait_send(), 0)[1], 0)
-    for k in range(1, S):
-        cnt_copy(k).wait_send()
+    for p in range(C):
+        @pl.when((r_other < C - 1) | (p < C - 1))
+        def _():
+            x_copy(p).wait_send()
+    for k in range(1, S):
         m1_copy(k).wait_send()
 
     lax.fori_loop(1, G, m2_wait, 0)
@@ -346,7 +442,7 @@
         outer = outer + w2[peer] * msgs2[peer]
     incoming = inner + outer * jnp.exp((s * T).astype(F32) * rates)
     smoothed = local + incoming * jnp.exp((step + 1.0) * rates)
-    prof_ref[...] = (smoothed * norm)[:2]
+    out_ref[1:3] = (smoothed * norm)[:2]
     lax.fori_loop(1, G, lambda k, _: (m2_copy(k).wait_send(), 0)[1], 0)
 
 
@@ -360,11 +456,11 @@
     def body(*refs):
         kernel_body(G, S, *refs)
 
-    ld, prof = pl.pallas_call(
+    out = pl.pallas_call(
         body,
-        out_shape=(jax.ShapeDtypeStruct((1, T), F32), jax.ShapeDtypeStruct((2, T), F32)),
+        out_shape=jax.ShapeDtypeStruct((8, T), F32),
         in_specs=[pl.BlockSpec(memory_space=pl.ANY), pl.BlockSpec(memory_space=pltpu.VMEM)],
-        out_specs=(pl.BlockSpec(memory_space=pltpu.VMEM), pl.BlockSpec(memory_space=pltpu.VMEM)),
+        out_specs=pl.BlockSpec(memory_space=pltpu.VMEM),
         scratch_shapes=[
             pltpu.VMEM((C, rows, T), BF16),
             pltpu.VMEM((rows, width), BF16),
@@ -372,6 +468,9 @@
             pltpu.VMEM((rows, T), BF16),
             pltpu.VMEM((C, C, T, T), BF16),
             pltpu.VMEM((RING, 2, C, T, T), BF16),
+            pltpu.VMEM((C, RING, 2, T, T), BF16),
+            pltpu.VMEM((RING, C, 2, T, T), BF16),
+            pltpu.VMEM((S, T, T), BF16),
             pltpu.VMEM((C, T, T), BF16),
             pltpu.VMEM((C, T, T), BF16),
             pltpu.VMEM((C, T, T), F32),
@@ -390,13 +489,13 @@
             pltpu.VMEM((S, 8, T), F32),
             pltpu.VMEM((G, 8, T), F32),
             dma((C,)), dma((C,)), dma((C,)), dma((S,)), dma((S,)), dma, dma,
-            dma((C, C)), dma((RING, 2, C)), dma((C,)), dma((C,)),
+            dma((C,)), dma((RING, 2)), dma((C, RING)), dma((RING, C)), dma, dma((S,)), dma((C,)), dma((C,)),
             dma((S,)), dma((S,)), dma((G,)), dma((G,)),
         ],
         compiler_params=pltpu.CompilerParams(collective_id=0, has_side_effects=True),
         name="ld_scores",
     )(haplotypes, window_ends.reshape(1, T))
-    return ld.reshape(T), prof
+    return out[0], out[1:3]
 
 
 def solution(mesh):

time: 109 us -> 89.3 us (0.82)
  Pallas kernels: 106 us -> 86.1 us
    pallas_call x1, Pallas kernels: 106 us -> 86.1 us  [per_device(): pl.pallas_call(body, out_shape=jax.ShapeDtypeStruct((8, T), F32), in_spec...]
    unnamed x2 -> x0, local copies, waits for them, and re-layouts: 2.36 us -> none
    slice x0 -> x1, local copies, waits for them, and re-layouts: none -> 1.25 us  [per_device(): return (out[0], out[1:3])]
    squeeze x0 -> x1, local copies, waits for them, and re-layouts: none -> 1.19 us  [per_device(): return (out[0], out[1:3])]
where the time goes in v2:
time: 89.3 us; the launch traced here: 89.1 us
  Pallas kernels  86.1 us (96%)
  local copies, waits for them, and re-layouts  2.44 us (3%)
    pallas_call x1, Pallas kernels, per_device(): pl.pallas_call(body, out_shape=jax.ShapeDtypeStruct((8, T), F32), in_spec...  86.1 us

profile of v2, /device:TPU:1, one launch (start us, length us, event | category | flops | bytes accessed | tf_op | source)
XLA Modules:
  0.0 89.1 jit_solution(11159860438936079799)
XLA Ops:
  0.6 86.1 %ld_scores.1 = f32[8,128]{1,0:T(8,128)} custom-call(bf16[2048,1024]{1,0:T(8,128)(2,1)} %refs_0_.1, s32[1,128]{1,0:T(1,128)} %bitcast.3), custom_call_target="tpu_custom_call" | custom-call | tf_op jit(solution)/shard_map/ld_scores/pallas_call | solution.py:459
  86.7 1.2 %slice_bitcast_fusion = f32[128]{0:T(128)} fusion(f32[8,128]{1,0:T(8,128)} %ld_scores.1), kind=kLoop, calls=%fused_computation | loop fusion | bytes 1024 | tf_op jit(solution)/shard_map/squeeze | solution.py:498
  87.9 1.2 %slice.7 = f32[2,128]{1,0:T(2,128)} slice(f32[8,128]{1,0:T(8,128)} %ld_scores.1), slice={[1:3], [0:128]} | slice | bytes 2048 | tf_op jit(solution)/shard_map/slice | solution.py:498

commit v3 on v2

--- a/solution.py
+++ b/solution.py
@@ -15,6 +15,7 @@
 FIRST = 2
 AHEAD = 2
 RING = 4
+PLANE = 4
 
 
 def rate_rows(shape, share, variants):
@@ -36,9 +37,9 @@
 def kernel_body(
     G, S, x_ref, ends_ref, out_ref,
     raw, xs, halo, hs, sb, yr, hb, yh, last, xsend, xrecv, diag, own, score,
-    cnt, cnts, tot, htot, stat, hstat, msg1, msgs1, msg2, msgs2, w1, w2,
+    cnt, cnts, tot, htot, stat, hstat, msg1, msgs1, msg2, msgs2, msg3, msgs3, w1, w2, w3, w4,
     load_sem, halo_s, halo_r, cnt_s, cnt_r, stat_s, stat_r,
-    y_s, y_r, h_s, h_r, d_s, d_r, x_s, x_r, m1_s, m1_r, m2_s, m2_r,
+    y_s, y_r, h_s, h_r, d_s, d_r, x_s, x_r, m1_s, m1_r, m2_s, m2_r, m3_s, m3_r,
 ):
     rows = x_ref.shape[0]
     width = x_ref.shape[1]
@@ -51,6 +52,9 @@
     half = s // RING
     partner = lax.rem(s + RING, S)
     before = lax.rem(g + G - 1, G)
+    Z = G // PLANE
+    z = g // PLANE
+    w = lax.rem(g, PLANE)
 
     barrier = pltpu.get_barrier_semaphore()
 
@@ -58,9 +62,8 @@
         pl.semaphore_signal(barrier, inc=1, device_id={"samples": lax.rem(s + k, S)}, device_id_type=MESH)
         return 0
 
-    def greet_g(k, _):
-        pl.semaphore_signal(barrier, inc=1, device_id={"genome": lax.rem(g + k, G)}, device_id_type=MESH)
-        return 0
+    def greet_g(to):
+        pl.semaphore_signal(barrier, inc=1, device_id={"genome": to}, device_id_type=MESH)
 
     def load(c):
         return pltpu.make_async_copy(x_ref.at[:, pl.ds(c * T, T)], raw.at[c], load_sem.at[c])
@@ -68,7 +71,12 @@
     for c in range(C):
         load(c).start()
     lax.fori_loop(1, S, greet_s, 0)
-    lax.fori_loop(1, G, greet_g, 0)
+    greet_g(before)
+    greet_g(lax.rem(g + 1, G))
+    for k in range(1, PLANE):
+        greet_g(z * PLANE + lax.rem(w + k, PLANE))
+    for k in range(1, Z):
+        greet_g(lax.rem(g + k * PLANE, G))
 
     ones = jnp.ones((16, rows), BF16)
     for c in range(C):
@@ -76,7 +84,7 @@
         sums = jnp.dot(ones, raw[c], preferred_element_type=F32)
         cnt[pl.ds(c, 1), :] = sums[0:1, :]
 
-    pl.semaphore_wait(barrier, S + G - 2)
+    pl.semaphore_wait(barrier, S + PLANE + Z - 1)
 
     def halo_copy(c):
         return pltpu.make_async_remote_copy(
@@ -110,18 +118,26 @@
 
     rates = rate_rows((8, T), T, variants)
 
+    def decayed(steps):
+        ahead = steps.astype(F32)
+        return jnp.where(ahead >= 0.0, jnp.exp(jnp.maximum(ahead, 0.0) * rates), 0.0)
+
     def weight1(k, _):
-        ahead = (s - 1 - k).astype(F32)
-        w1[k] = jnp.where(ahead >= 0.0, jnp.exp(jnp.maximum(ahead, 0.0) * T * rates), 0.0)
+        w1[k] = decayed((s - 1 - k) * T)
+        w4[k] = decayed((S - 1 - k) * T)
         return 0
 
     def weight2(k, _):
-        ahead = (g - 1 - k).astype(F32)
-        w2[k] = jnp.where(ahead >= 0.0, jnp.exp(jnp.maximum(ahead, 0.0) * width * rates), 0.0)
+        w2[k] = decayed(jnp.where(k < z, ((z - k) * PLANE - 1 - w) * width, -1))
+        return 0
+
+    def weight3(k, _):
+        w3[k] = decayed((w - 1 - k) * width)
         return 0
 
     lax.fori_loop(0, S, weight1, 0)
-    lax.fori_loop(0, G, weight2, 0)
+    lax.fori_loop(0, Z, weight2, 0)
+    lax.fori_loop(0, PLANE, weight3, 0)
 
     total = cnt[...]
     for k in range(1, S):
@@ -187,17 +203,7 @@
             device_id={"samples": half * RING + slot}, device_id_type=MESH,
         )
 
-    def d_copy():
-        return pltpu.make_async_remote_copy(
-            src_ref=hb.at[C - 1, RING - 1, 1], dst_ref=last.at[s], send_sem=d_s, recv_sem=d_r.at[s],
-            device_id={"samples": S - 1}, device_id_type=MESH,
-        )
-
-    def d_arrival(k):
-        return pltpu.make_async_remote_copy(
-            src_ref=hb.at[C - 1, RING - 1, 1], dst_ref=last.at[k], send_sem=d_s, recv_sem=d_r.at[k],
-            device_id={"samples": k}, device_id_type=MESH,
-        )
+    d_copy, d_arrival = to_samples(hb.at[C - 1, RING - 1, 1], last, d_s, d_r)
 
     B = 2
     for q in range(C // B):
@@ -270,12 +276,15 @@
         return 0
 
     def add_squares(p, value):
+        score[...] += squares(r_own, p, value, ends_ref[...] - g * width)
+
+    def squares(r, p, value, end):
         value = value * (1.0 / haplos)
-        row = r_own * T + lane
+        row = r * T + lane
         col = p * T + sub
-        end = jnp.broadcast_to(ends_ref[...] - g * width, (T, T))
+        end = jnp.broadcast_to(end, (T, T))
         inside = ((col > row) & (col < end)) | ((col < row) & (col + width < end))
-        score[...] += jnp.sum(jnp.where(inside, value * value, 0.0), axis=0, keepdims=True)
+        return jnp.sum(jnp.where(inside, value * value, 0.0), axis=0, keepdims=True)
 
     score[...] = jnp.zeros_like(score)
 
@@ -298,9 +307,8 @@
         for r in range(c + 1, C):
             hb[c, r % RING, r // RING] = product[:, (r - c) * T : (r - c + 1) * T].astype(BF16)
         if c == C - 1:
-            @pl.when(s != S - 1)
-            def _():
-                d_copy().start()
+            for k in range(1, S):
+                d_copy(k).start()
             return
         for to in range(RING):
             if c <= to + RING:
@@ -326,7 +334,7 @@
             finish_tile(c, 0)
 
     SELF_AT = 3
-    for c in range(C):
+    for c in range(C - 1):
         halo_chunk(c)
         if c == SELF_AT:
             self_wait(1 - half)
@@ -337,35 +345,79 @@
                 halo_sums(k)
         elif c > SELF_AT:
             halo_sums(c - 1)
-        if c == SELF_AT + 1:
-            lax.fori_loop(r_own + 1, C, finish_tile, 0)
-            for k in range(SELF_AT):
-                halo_finish(k)
-        elif c > SELF_AT + 1:
-            halo_finish(c - 2)
-    halo_finish(C - 2)
-
-    @pl.when(s == S - 1)
-    def _():
-        value = hb[C - 1, RING - 1, 1].astype(F32)
-        for k in range(S - 1):
-            d_arrival(k).wait_recv()
-        for k in range(S - 1):
-            value = value + last[k].astype(F32)
-        add_squares(C - 1, value)
-
-    row = r_own * T + lax.broadcasted_iota(jnp.int32, (1, T), 1)
-    counted = jnp.maximum(ends_ref[...] - g * width - row - 1, 1).astype(F32)
-    ld = score[...] / counted
+    halo_sums(C - 2)
+    lax.fori_loop(r_own + 1, C, finish_tile, 0)
+    for c in range(SELF_AT):
+        halo_finish(c)
+    halo_chunk(C - 1)
+    for c in range(SELF_AT, C - 1):
+        halo_finish(c)
+
+    step = lax.broadcasted_iota(jnp.int32, (8, T), 1).astype(F32)
+    tail = jnp.exp((T - 1.0 - step) * rates)
+
+    def scores(squared, r, end):
+        row = r * T + lax.broadcasted_iota(jnp.int32, (1, T), 1)
+        return squared / jnp.maximum(end - row - 1, 1).astype(F32)
+
+    def decayed_sum(values):
+        return jnp.broadcast_to(jnp.sum(values * tail, axis=1, keepdims=True), (8, T))
+
+    end = ends_ref[...] - g * width
+    early = scores(score[...], r_own, end)
+    msg1[0] = decayed_sum(early)
+    msg1[1] = jnp.broadcast_to(score[...], (8, T))
+    msg1[2] = jnp.broadcast_to(end.astype(F32), (8, T))
+    m1_copy, m1_arrival = to_samples(msg1, msgs1, m1_s, m1_r)
+    for k in range(1, S):
+        m1_copy(k).start()
+    msgs1[s] = msg1[...]
+
+    value = hb[C - 1, RING - 1, 1].astype(F32)
+    for k in range(1, S):
+        d_arrival(k).wait_recv()
+    for k in range(1, S):
+        value = value + last[lax.rem(s + k, S)].astype(F32)
+    for k in range(1, S):
+        m1_arrival(k).wait_recv()
+    last_end = msgs1[S - 1, 2, 0:1, :].astype(jnp.int32)
+    last_squared = msgs1[S - 1, 1, 0:1, :] + squares(S - 1, C - 1, value, last_end)
+    last_ld = scores(last_squared, S - 1, last_end)
+    whole = decayed_sum(last_ld)
+    inner = jnp.zeros((8, T), F32)
+    for k in range(S - 1):
+        inner = inner + w1[k] * msgs1[k, 0]
+        whole = whole + w4[k] * msgs1[k, 0]
+    msg2[...] = whole
+
+    def to_genome(src, dst, ss, rs, slot, place):
+        def copy(k):
+            return pltpu.make_async_remote_copy(
+                src_ref=src, dst_ref=dst.at[slot(0)], send_sem=ss.at[k], recv_sem=rs.at[slot(0)],
+                device_id={"genome": place(k)}, device_id_type=MESH,
+            )
+
+        def arrival(k):
+            return pltpu.make_async_remote_copy(
+                src_ref=src, dst_ref=dst.at[slot(k)], send_sem=ss.at[k], recv_sem=rs.at[slot(k)],
+                device_id={"genome": place(k)}, device_id_type=MESH,
+            )
+
+        return copy, arrival
+
+    m2_copy, m2_arrival = to_genome(
+        msg2, msgs2, m2_s, m2_r, lambda k: lax.rem(z + k, Z), lambda k: lax.rem(g + k * PLANE, G)
+    )
+    m3_copy, m3_arrival = to_genome(
+        msg3, msgs3, m3_s, m3_r, lambda k: lax.rem(w + k, PLANE),
+        lambda k: z * PLANE + lax.rem(w + k, PLANE),
+    )
+    for k in range(1, Z):
+        m2_copy(k).start()
+    msg3[1] = whole
+
+    ld = jnp.where(s == S - 1, last_ld, early)
     out_ref[0:1] = ld
-    step = lax.broadcasted_iota(jnp.int32, (8, T), 1).astype(F32)
-    msg1[...] = jnp.broadcast_to(
-        jnp.sum(ld * jnp.exp((T - 1.0 - step) * rates), axis=1, keepdims=True), (8, T)
-    )
-    m1_copy, m1_arrival = to_samples(msg1, msgs1, m1_s, m1_r)
-    for k in range(1, S):
-        m1_copy(k).start()
-
     lag = (lane - sub).astype(F32)
     locals_ = []
     for rate in (math.log(0.5) / (4 * T), math.log(0.1) / variants):
@@ -377,38 +429,15 @@
     place = (g * width + s * T + 1).astype(F32) + step
     norm = one_minus_exp(rates) / one_minus_exp(place * rates)
 
-    for k in range(1, S):
-        m1_arrival(k).wait_recv()
-    inner = w1[s] * msg1[...]
-    whole = msg1[...] * jnp.exp((S - 1 - s).astype(F32) * T * rates)
-    for k in range(1, S):
-        peer = lax.rem(s + k, S)
-        inner = inner + w1[peer] * msgs1[peer]
-        whole = whole + msgs1[peer] * jnp.exp((S - 1 - peer).astype(F32) * T * rates)
-    msg2[...] = whole
-
-    def m2_copy(k):
-        return pltpu.make_async_remote_copy(
-            src_ref=msg2, dst_ref=msgs2.at[g], send_sem=m2_s.at[k], recv_sem=m2_r.at[g],
-            device_id={"genome": lax.rem(g + k, G)}, device_id_type=MESH,
-        )
-
-    def m2_arrival(k):
-        peer = lax.rem(g + k, G)
-        return pltpu.make_async_remote_copy(
-            src_ref=msg2, dst_ref=msgs2.at[peer], send_sem=m2_s.at[k], recv_sem=m2_r.at[peer],
-            device_id={"genome": peer}, device_id_type=MESH,
-        )
-
-    def m2_start(k, _):
-        m2_copy(k).start()
-        return 0
-
-    def m2_wait(k, _):
+    outer = jnp.zeros((8, T), F32)
+    for k in range(1, Z):
         m2_arrival(k).wait_recv()
-        return 0
-
-    lax.fori_loop(1, G, m2_start, 0)
+    for k in range(1, Z):
+        peer = lax.rem(z + k, Z)
+        outer = outer + w2[peer] * msgs2[peer]
+    msg3[0] = outer
+    for k in range(1, PLANE):
+        m3_copy(k).start()
 
     for c in range(C - AHEAD, C):
         halo_copy(c).wait_send()
@@ -423,10 +452,6 @@
                 if c <= to + RING:
                     h_copy(c, to).wait_send()
 
-    @pl.when(s != S - 1)
-    def _():
-        d_copy().wait_send()
-
     stat_copy.wait_send()
     for p in range(C):
         @pl.when((r_other < C - 1) | (p < C - 1))
@@ -434,16 +459,28 @@
             x_copy(p).wait_send()
     for k in range(1, S):
         m1_copy(k).wait_send()
-
-    lax.fori_loop(1, G, m2_wait, 0)
-    outer = jnp.zeros((8, T), F32)
-    for k in range(1, G):
-        peer = lax.rem(g + k, G)
-        outer = outer + w2[peer] * msgs2[peer]
+        d_copy(k).wait_send()
+    for k in range(1, Z):
+        m2_copy(k).wait_send()
+
+    for k in range(1, PLANE):
+        m3_arrival(k).wait_recv()
+    beside = jnp.zeros((8, T), F32)
+    for k in range(1, PLANE):
+        peer = lax.rem(w + k, PLANE)
+        outer = outer + msgs3[peer, 0]
+        beside = beside + w3[peer] * msgs3[peer, 1]
+    outer = outer * jnp.exp((w * width).astype(F32) * rates) + beside
     incoming = inner + outer * jnp.exp((s * T).astype(F32) * rates)
     smoothed = local + incoming * jnp.exp((step + 1.0) * rates)
     out_ref[1:3] = (smoothed * norm)[:2]
-    lax.fori_loop(1, G, lambda k, _: (m2_copy(k).wait_send(), 0)[1], 0)
+    for k in range(1, PLANE):
+        m3_copy(k).wait_send()
+
+
+def split_rows(all_ref, ld_ref, prof_ref):
+    ld_ref[...] = all_ref[0:1]
+    prof_ref[...] = all_ref[1:3]
 
 
 def per_device(haplotypes, window_ends):
@@ -451,6 +488,7 @@
     S = lax.axis_size("samples")
     rows, width = haplotypes.shape
     C = width // T
+    Z = G // PLANE
     dma = pltpu.SemaphoreType.DMA
 
     def body(*refs):
@@ -482,20 +520,29 @@
             pltpu.VMEM((8, T), F32),
             pltpu.VMEM((2, 8, T), F32),
             pltpu.VMEM((2, 8, T), F32),
+            pltpu.VMEM((3, 8, T), F32),
+            pltpu.VMEM((S, 3, 8, T), F32),
             pltpu.VMEM((8, T), F32),
+            pltpu.VMEM((Z, 8, T), F32),
+            pltpu.VMEM((2, 8, T), F32),
+            pltpu.VMEM((PLANE, 2, 8, T), F32),
             pltpu.VMEM((S, 8, T), F32),
-            pltpu.VMEM((8, T), F32),
-            pltpu.VMEM((G, 8, T), F32),
+            pltpu.VMEM((Z, 8, T), F32),
+            pltpu.VMEM((PLANE, 8, T), F32),
             pltpu.VMEM((S, 8, T), F32),
-            pltpu.VMEM((G, 8, T), F32),
             dma((C,)), dma((C,)), dma((C,)), dma((S,)), dma((S,)), dma, dma,
-            dma((C,)), dma((RING, 2)), dma((C, RING)), dma((RING, C)), dma, dma((S,)), dma((C,)), dma((C,)),
-            dma((S,)), dma((S,)), dma((G,)), dma((G,)),
+            dma((C,)), dma((RING, 2)), dma((C, RING)), dma((RING, C)), dma((S,)), dma((S,)), dma((C,)), dma((C,)),
+            dma((S,)), dma((S,)), dma((Z,)), dma((Z,)), dma((PLANE,)), dma((PLANE,)),
         ],
         compiler_params=pltpu.CompilerParams(collective_id=0, has_side_effects=True),
         name="ld_scores",
     )(haplotypes, window_ends.reshape(1, T))
-    return out[0], out[1:3]
+    ld, profile = pl.pallas_call(
+        split_rows,
+        out_shape=(jax.ShapeDtypeStruct((1, T), F32), jax.ShapeDtypeStruct((2, T), F32)),
+        name="outputs",
+    )(out)
+    return ld.reshape(T), profile
 
 
 def solution(mesh):

time: 89.3 us -> 84.5 us (0.946)
  local copies, waits for them, and re-layouts: 2.44 us -> 0 us
  Pallas kernels: 86.1 us -> 83.8 us
    pallas_call x1, Pallas kernels: 86.1 us -> 82.5 us  [per_device(): pl.pallas_call(body, out_shape=jax.ShapeDtypeStruct((8, T), F32), in_spec...]
    slice x1 -> x0, local copies, waits for them, and re-layouts: 1.25 us -> none  [per_device(): return (out[0], out[1:3])]
    pallas_call x0 -> x1, Pallas kernels: none -> 1.24 us  [per_device(): pl.pallas_call(split_rows, out_shape=(jax.ShapeDtypeStruct((1, T), F32),...]
    squeeze x1 -> x0, local copies, waits for them, and re-layouts: 1.19 us -> none  [per_device(): return (out[0], out[1:3])]
where the time goes in v3:
time: 84.5 us; the launch traced here: 84.4 us
  Pallas kernels  83.8 us (99%)
    pallas_call x1, Pallas kernels, per_device(): pl.pallas_call(body, out_shape=jax.ShapeDtypeStruct((8, T), F32), in_spec...  82.5 us

profile of v3, /device:TPU:1, one launch (start us, length us, event | category | flops | bytes accessed | tf_op | source)
XLA Modules:
  0.0 84.4 jit_solution(10547691575218938786)
XLA Ops:
  0.6 82.5 %ld_scores.1.all_ref = f32[8,128]{1,0:T(8,128)} custom-call(bf16[2048,1024]{1,0:T(8,128)(2,1)} %refs_0_.1, s32[1,128]{1,0:T(1,128)} %bitcast.2), custom_call_target="tpu_custom_call" | custom-call | tf_op jit(solution)/shard_map/ld_scores/pallas_call | solution.py:497
  83.2 1.2 %outputs.1 = (f32[1,128]{1,0:T(1,128)}, f32[2,128]{1,0:T(2,128)}) custom-call(f32[8,128]{1,0:T(8,128)} %ld_scores.1.all_ref), custom_call_target="tpu_custom_call" | custom-call | tf_op jit(solution)/shard_map/outputs/pallas_call | solution.py:540

commit v4 on v3

--- a/solution.py
+++ b/solution.py
@@ -36,7 +36,7 @@
 
 def kernel_body(
     G, S, x_ref, ends_ref, out_ref,
-    raw, xs, halo, hs, sb, yr, hb, yh, last, xsend, xrecv, diag, own, score,
+    raw, xs, halo, hs, sb, yr, hb, yh, last, xsend, xrecv, xfine, xfiner, diag, own, score,
     cnt, cnts, tot, htot, stat, hstat, msg1, msgs1, msg2, msgs2, msg3, msgs3, w1, w2, w3, w4,
     load_sem, halo_s, halo_r, cnt_s, cnt_r, stat_s, stat_r,
     y_s, y_r, h_s, h_r, d_s, d_r, x_s, x_r, m1_s, m1_r, m2_s, m2_r, m3_s, m3_r,
@@ -224,8 +224,7 @@
             value = value + yr[lax.rem(y + k, RING), j, p].astype(F32)
         return value
 
-    def halo_sum(j, c):
-        value = hb[c, y, j].astype(F32)
+    def halo_sum(j, c, value):
         for k in range(1, RING):
             value = value + yh[lax.rem(y + k, RING), c, j].astype(F32)
         return value
@@ -255,6 +254,12 @@
     def x_copy(p):
         return pltpu.make_async_remote_copy(
             src_ref=xsend.at[p], dst_ref=xrecv.at[p], send_sem=x_s.at[p], recv_sem=x_r.at[p],
+            device_id={"samples": partner}, device_id_type=MESH,
+        )
+
+    def fine_copy(p):
+        return pltpu.make_async_remote_copy(
+            src_ref=xfine, dst_ref=xfiner, send_sem=x_s.at[p], recv_sem=x_r.at[p],
             device_id={"samples": partner}, device_id_type=MESH,
         )
 
@@ -303,6 +308,7 @@
             hs[pl.ds(b * STEP, STEP), :] = ((part - f) * d).astype(BF16)
         product = transposed_dot(hs[...], xs[:, c * T :])
         first = jnp.where(sub > lane, diag[c], product[:, :T])
+        diag[c] = first
         hb[c, c % RING, c // RING] = first.astype(BF16)
         for r in range(c + 1, C):
             hb[c, r % RING, r // RING] = product[:, (r - c) * T : (r - c + 1) * T].astype(BF16)
@@ -319,21 +325,36 @@
     def halo_sums(c):
         halo_wait(c)
 
-        @pl.when(r_other >= c)
-        def _():
-            xsend[c] = halo_sum(1 - half, c).astype(BF16)
+        @pl.when(r_other > c)
+        def _():
+            xsend[c] = halo_sum(1 - half, c, hb[c, y, 1 - half].astype(F32)).astype(BF16)
             x_copy(c).start()
 
-        @pl.when(r_own >= c)
-        def _():
-            own[c] = halo_sum(half, c)
+        @pl.when(r_other == c)
+        def _():
+            xfine[...] = halo_sum(1 - half, c, diag[c])
+            fine_copy(c).start()
+
+        @pl.when(r_own > c)
+        def _():
+            own[c] = halo_sum(half, c, hb[c, y, half].astype(F32))
+
+        @pl.when(r_own == c)
+        def _():
+            own[c] = halo_sum(half, c, diag[c])
 
     def halo_finish(c):
-        @pl.when(r_own >= c)
+        @pl.when(r_own > c)
         def _():
             finish_tile(c, 0)
 
-    SELF_AT = 3
+        @pl.when(r_own == c)
+        def _():
+            fine_copy(c).wait_recv()
+            add_squares(c, own[c] + xfiner[...])
+
+    SELF_AT = 2
+    FINISH_AT = 4
     for c in range(C - 1):
         halo_chunk(c)
         if c == SELF_AT:
@@ -347,10 +368,10 @@
             halo_sums(c - 1)
     halo_sums(C - 2)
     lax.fori_loop(r_own + 1, C, finish_tile, 0)
-    for c in range(SELF_AT):
+    for c in range(FINISH_AT):
         halo_finish(c)
     halo_chunk(C - 1)
-    for c in range(SELF_AT, C - 1):
+    for c in range(FINISH_AT, C - 1):
         halo_finish(c)
 
     step = lax.broadcasted_iota(jnp.int32, (8, T), 1).astype(F32)
@@ -373,7 +394,7 @@
         m1_copy(k).start()
     msgs1[s] = msg1[...]
 
-    value = hb[C - 1, RING - 1, 1].astype(F32)
+    value = diag[C - 1]
     for k in range(1, S):
         d_arrival(k).wait_recv()
     for k in range(1, S):
@@ -454,9 +475,14 @@
 
     stat_copy.wait_send()
     for p in range(C):
-        @pl.when((r_other < C - 1) | (p < C - 1))
+        @pl.when(r_other != p)
         def _():
             x_copy(p).wait_send()
+
+        if p < C - 1:
+            @pl.when(r_other == p)
+            def _():
+                fine_copy(p).wait_send()
     for k in range(1, S):
         m1_copy(k).wait_send()
         d_copy(k).wait_send()
@@ -511,6 +537,8 @@
             pltpu.VMEM((S, T, T), BF16),
             pltpu.VMEM((C, T, T), BF16),
             pltpu.VMEM((C, T, T), BF16),
+            pltpu.VMEM((T, T), F32),
+            pltpu.VMEM((T, T), F32),
             pltpu.VMEM((C, T, T), F32),
             pltpu.VMEM((C, T, T), F32),
             pltpu.VMEM((1, T), F32),

time: 84.5 us -> 85.2 us (level)
  no operation moved by 1% of the time
where the time goes in v4:
time: 85.2 us; the launch traced here: 85.1 us
  Pallas kernels  84.5 us (99%)
    pallas_call x1, Pallas kernels, per_device(): pl.pallas_call(body, out_shape=jax.ShapeDtypeStruct((8, T), F32), in_spec...  83.2 us

profile of v4, /device:TPU:1, one launch (start us, length us, event | category | flops | bytes accessed | tf_op | source)
XLA Modules:
  0.0 85.1 jit_solution(1220515509659335459)
XLA Ops:
  0.6 83.2 %ld_scores.1.all_ref = f32[8,128]{1,0:T(8,128)} custom-call(bf16[2048,1024]{1,0:T(8,128)(2,1)} %refs_0_.1, s32[1,128]{1,0:T(1,128)} %bitcast.2), custom_call_target="tpu_custom_call" | custom-call | tf_op jit(solution)/shard_map/ld_scores/pallas_call | solution.py:523
  83.9 1.2 %outputs.1 = (f32[1,128]{1,0:T(1,128)}, f32[2,128]{1,0:T(2,128)}) custom-call(f32[8,128]{1,0:T(8,128)} %ld_scores.1.all_ref), custom_call_target="tpu_custom_call" | custom-call | tf_op jit(solution)/shard_map/outputs/pallas_call | solution.py:568
